TPU v7x, 32 devices: a whole 2x2x4 slice. The times are simulated.
32 devices in a mesh: section: 4 (over z), expert: 4 (over y, x), dp: 2 (over core).
Axes of the slice: x: 2, y: 2, z: 4, core: 2. Of those that a mesh axis runs over, the one named last changes fastest.
Arguments:
- stash: bfloat16 [4, 256, 2048], P('section', 'dp', 'expert'), may hold values from -6 to 6
- cotangent: bfloat16 [4, 256, 2048], P('section', 'dp', 'expert'), may hold values from -6 to 6
- backward_expert_routes: int32 [4, 256, 2], P('section', 'dp'), may hold values from 0 to 3, all different within a row; in each aligned block of 128 rows (0 to 127, 128 to 255, ..., all dimensions but the last counted through in order) at most 80 rows name the same one
- backward_job_lengths: int32 [4, 4], P('section'), may hold values from 1 to 128, 256 in all within a row
- layer_norm_gains: float32 [4, 2048], P('section'), may hold values from 0.25 to 1.75
- router: bfloat16 [4, 2048, 4], P('section'), may hold values from -0.125 to 0.125
- expert_gate_weight: bfloat16 [4, 2048, 28672], P('section', None, ('expert', 'dp')), may hold values from -0.125 to 0.125
- expert_up_weight: bfloat16 [4, 2048, 28672], P('section', None, ('expert', 'dp')), may hold values from -0.125 to 0.125
- expert_down_weight: bfloat16 [4, 28672, 2048], P('section', ('expert', 'dp')), may hold values from -0.0625 to 0.0625
- adapter_down_maps: bfloat16 [4, 2048, 64], P('section', 'expert'), may hold values from -0.125 to 0.125
- adapter_up_maps: bfloat16 [4, 64, 2048], P('section', None, 'expert'), may hold values from -1.5 to 1.5
Outputs:
- handed_back: bfloat16 [4, 256, 2048], P('section', 'dp', 'expert')
- grad_lora_down: float32 [4, 2048, 64], P('section', 'expert')
- grad_lora_up: float32 [4, 64, 2048], P('section', None, 'expert')
Inputs may be any that keep to these rules, and one draw needn't show every extreme that they name: `backward_expert_routes`: each row names two different experts. In each aligned block of 128 rows (the tokens of one device) no expert is named more than 80 times. `backward_job_lengths`: each row sums to 256.
All inputs are finite; a program needn't handle non-finite values.
Results may differ from a plain program's by a relative error of at most 0.008.
Values may be sent and summed in bfloat16 or wider, within the bound.
A program may use at most 128 MiB of HBM per device.

v0:
```python
import jax
import jax.numpy as jnp
from jax import lax
from jax.sharding import PartitionSpec as P

MODEL_WIDTH = 2048
EXPERTS = 4
ADAPTER_RANK = 16
CAP = 80
EPS = 1e-05
ADAPTER_SCALE = 0.5
HIGH = lax.Precision.HIGHEST


def from_behind(block, axis, distance):
    devices = range(lax.axis_size(axis))
    route = [((i - distance) % len(devices), i) for i in devices]
    return lax.ppermute(block, axis, route)


def job_columns(job_token_lengths, offset, count):
    ends = jnp.cumsum(job_token_lengths, dtype=jnp.int32)
    position = offset + jnp.arange(count, dtype=jnp.int32)
    owner = jnp.sum((ends[None, :] <= position[:, None]).astype(jnp.int32), axis=1, dtype=jnp.int32)
    column_owner = (
        jnp.arange(job_token_lengths.shape[0] * ADAPTER_RANK, dtype=jnp.int32) // ADAPTER_RANK
    )
    return (owner[:, None] == column_owner[None, :]).astype(jnp.float32)


def prepare(whole_batch, norm_gain_vector, router, token_routes):
    expert_values = whole_batch.astype(jnp.float32)
    scale = lax.rsqrt(jnp.mean(expert_values * expert_values, axis=1, keepdims=True) + EPS)
    normalized_input = (expert_values * scale * norm_gain_vector[None, :]).astype(jnp.bfloat16)
    logits = jnp.dot(normalized_input, router, preferred_element_type=jnp.float32)
    labels = jnp.arange(router.shape[1], dtype=jnp.int32)
    first = (token_routes[:, 0:1] == labels[None, :]).astype(jnp.float32)
    second = (token_routes[:, 1:2] == labels[None, :]).astype(jnp.float32)
    upper = jax.nn.sigmoid(jnp.sum(first * logits, axis=1) - jnp.sum(second * logits, axis=1))
    table = upper[:, None] * first + (1.0 - upper)[:, None] * second
    return (expert_values, scale, normalized_input, first, second, upper, table)


def router_grad(gate_grad, first, second, upper):
    spread = jnp.sum(first * gate_grad, axis=1) - jnp.sum(second * gate_grad, axis=1)
    delta = spread * upper * (1.0 - upper)
    return delta[:, None] * (first - second)


def slot_matrix(member, capacity):
    marks = member.astype(jnp.int32)
    ranked = jnp.cumsum(marks, axis=-1, dtype=jnp.int32) - marks
    slots = jnp.arange(capacity, dtype=jnp.int32)
    hit = (ranked[..., None, :] == slots[:, None]) & (marks[..., None, :] == 1)
    return hit.astype(jnp.float32)


def expert_back(
    rows, adapter_gradient_list, expert_gate_weight, expert_up_weight, expert_down_weight
):
    gate = jnp.dot(rows, expert_gate_weight, preferred_element_type=jnp.float32)
    up = jnp.dot(rows, expert_up_weight, preferred_element_type=jnp.float32)
    sig = jax.nn.sigmoid(gate)
    act = gate * sig
    hidden = (act * up).astype(jnp.bfloat16)
    output = jnp.dot(hidden, expert_down_weight, preferred_element_type=jnp.float32)
    gate_term = jnp.sum(adapter_gradient_list.astype(jnp.float32) * output, axis=1)
    back = jnp.dot(adapter_gradient_list, expert_down_weight.T, preferred_element_type=jnp.float32)
    d_gate = (back * up * sig * (1.0 + gate * (1.0 - sig))).astype(jnp.bfloat16)
    d_up = (back * act).astype(jnp.bfloat16)
    d_rows = jnp.dot(d_gate, expert_gate_weight.T, preferred_element_type=jnp.float32) + jnp.dot(
        d_up, expert_up_weight.T, preferred_element_type=jnp.float32
    )
    return (d_rows, gate_term)


def body(
    stash,
    cotangent,
    backward_expert_routes,
    backward_job_lengths,
    layer_norm_gains,
    router,
    expert_gate_weight,
    expert_up_weight,
    expert_down_weight,
    adapter_down_maps,
    adapter_up_maps,
):
    groups = lax.axis_size("expert")
    shards = lax.axis_size("dp")
    column_block = lax.axis_index("expert")
    token_block = lax.axis_index("dp")
    mine = column_block // (groups // EXPERTS)
    s_cols = stash[0]
    gradient_columns = cotangent[0]
    count, width = s_cols.shape
    s_full, g_full = (
        lax.all_gather(s_cols, "expert", axis=1, tiled=True),
        lax.all_gather(gradient_columns, "expert", axis=1, tiled=True),
    )
    norm_gain_vector = layer_norm_gains[0]
    route_w = router[0]
    wg = expert_gate_weight[0]
    wu = expert_up_weight[0]
    wd = expert_down_weight[0]
    down_map_rows = adapter_down_maps[0]
    backward_columns = adapter_up_maps[0]
    col_start = column_block * width
    gain_cols = lax.dynamic_slice_in_dim(norm_gain_vector, col_start, width, 0)
    route_cols = lax.dynamic_slice_in_dim(route_w, col_start, width, 0)
    offset = token_block * count
    backward_mask = job_columns(backward_job_lengths[0], offset, count)
    b_values, b_scale, b_normed, b_first, b_second, b_upper, b_table = prepare(
        s_full, norm_gain_vector, route_w, backward_expert_routes[0]
    )
    labels = jnp.arange(EXPERTS, dtype=jnp.int32)
    own = (labels == mine).astype(jnp.float32)
    b_member = jnp.sum((b_first + b_second) * own[None, :], axis=1)
    b_gate = jnp.sum(b_table * own[None, :], axis=1)
    b_slots = slot_matrix(b_member, CAP)
    b_normed_cols = lax.dynamic_slice_in_dim(b_normed, col_start, width, 1)
    a_full = lax.all_gather(down_map_rows, "expert", axis=0, tiled=True)
    b_low = jnp.dot(b_normed, a_full, preferred_element_type=jnp.float32)
    grad_low_rank = lax.psum(
        jnp.dot(gradient_columns, backward_columns.T, preferred_element_type=jnp.float32), "expert"
    )
    backward_low_rank = (b_low * backward_mask).astype(jnp.bfloat16)
    grad_low_rank_backward = (ADAPTER_SCALE * grad_low_rank * backward_mask).astype(jnp.bfloat16)
    up_map_gradient = ADAPTER_SCALE * jnp.dot(
        backward_low_rank.T, gradient_columns, preferred_element_type=jnp.float32
    )
    down_map_gradient = jnp.dot(
        b_normed_cols.T, grad_low_rank_backward, preferred_element_type=jnp.float32
    )
    down_map_gradient, up_map_gradient = lax.psum((down_map_gradient, up_map_gradient), "dp")
    normalized_grad_adapter = jnp.dot(
        grad_low_rank_backward, down_map_rows.T, preferred_element_type=jnp.float32
    )
    b_slots_low = b_slots.astype(jnp.bfloat16)
    b_sel = jnp.dot(b_slots_low, b_normed, preferred_element_type=jnp.float32).astype(jnp.bfloat16)
    g_sel = jnp.dot(b_slots_low, g_full, preferred_element_type=jnp.float32).astype(jnp.bfloat16)
    b_rows, g_rows = (
        lax.all_gather(b_sel, "dp", axis=0, tiled=True),
        lax.all_gather(g_sel, "dp", axis=0, tiled=True),
    )
    dn_slots, dgam_slots = expert_back(b_rows, g_rows, wg, wu, wd)
    b_member_all, b_gate_all = (
        lax.all_gather(b_member, "dp", axis=0, tiled=True),
        lax.all_gather(b_gate, "dp", axis=0, tiled=True),
    )
    b_all = slot_matrix(b_member_all.reshape(shards, count), CAP)
    b_terms = jnp.einsum(
        "pct,pcex->eptx", b_all, dn_slots.reshape(shards, CAP, groups, width), precision=HIGH
    )
    b_terms = b_terms * b_gate_all.reshape(shards, count)[None, :, :, None]
    normalized_grad_experts = lax.psum_scatter(
        b_terms.reshape(groups * shards * count, width),
        ("expert", "dp"),
        scatter_dimension=0,
        tiled=True,
    )
    dgam_own = lax.psum_scatter(dgam_slots, "dp", scatter_dimension=0, tiled=True)
    dgam_tokens = jnp.dot(dgam_own, b_slots, precision=HIGH)
    gate_part = dgam_tokens[:, None] * own[None, :]
    expert_base_output = normalized_grad_experts + normalized_grad_adapter
    b_values_cols = lax.dynamic_slice_in_dim(b_values, col_start, width, 1)
    route_cols_t = route_cols.astype(jnp.float32).T
    base_weighted = expert_base_output * gain_cols[None, :]
    stat_part = jnp.sum(base_weighted * b_values_cols, axis=1, keepdims=True)
    gate_grad, stat_part = lax.psum((gate_part, stat_part), "expert")
    d_logit = router_grad(gate_grad, b_first, b_second, b_upper)
    lifted = jnp.dot(
        b_values * norm_gain_vector[None, :], route_w.astype(jnp.float32), precision=HIGH
    )
    stat = stat_part + jnp.sum(d_logit * lifted, axis=1, keepdims=True)
    weighted = base_weighted + jnp.dot(d_logit, route_cols_t, precision=HIGH) * gain_cols[None, :]
    layer_result = (
        gradient_columns.astype(jnp.float32)
        + b_scale * weighted
        - b_values_cols * b_scale * b_scale * b_scale * stat / MODEL_WIDTH
    )
    handed_back = from_behind(layer_result.astype(jnp.bfloat16), "section", -1)
    return (handed_back[None], down_map_gradient[None], up_map_gradient[None])


def solution(mesh):
    return jax.shard_map(
        body,
        mesh=mesh,
        in_specs=(
            P("section", "dp", "expert"),
            P("section", "dp", "expert"),
            P("section", "dp", None),
            P("section", None),
            P("section", None),
            P("section", None, None),
            P("section", None, ("expert", "dp")),
            P("section", None, ("expert", "dp")),
            P("section", ("expert", "dp"), None),
            P("section", "expert", None),
            P("section", None, "expert"),
        ),
        out_specs=(
            P("section", "dp", "expert"),
            P("section", "expert", None),
            P("section", None, "expert"),
        ),
        check_vma=False,
    )
```

profile of v0, /device:TPU:0, one launch (start us, length us, event | category | flops | bytes accessed | tf_op | source)
XLA Modules:
  0.0 168.8 jit_solution(5793704472606777799)
XLA Ops:
  8.0 0.0 copy-start
  8.0 0.0 copy-start.2
  8.0 0.0 reduce-scatter.2.cloned.1.call-start
  8.1 12.0 %all-gather = bf16[1,128,2048]{2,1,0:T(8,128)(2,1)S(1)} all-gather(bf16[1,128,512]{2,1,0:T(8,128)(2,1)} %param.11), channel_id=2, replica_groups=mesh['section'=4,'expert'=4,'dp'=2] {'expert'}, dimensions={2}, use_global_device_ids=true | all-gather | bytes 655360 | tf_op jit(solution)/shard_map/all_gather | solution.py:99
  20.1 0.2 fusion.33
  20.3 0.8 slice_bitcast_fusion.1
  21.0 0.9 fusion.35
  21.9 1.0 select_reduce_fusion.2
  22.9 0.1 multiply_reduce_fusion
  23.0 1.8 %all-gather.3 = f32[2,1,128]{2,1,0:T(1,128)S(1)} all-gather(f32[1,1,128]{2,1,0:T(1,128)S(1)} %bitcast.144), channel_id=1, replica_groups=mesh['section'=4,'expert'=4,'dp'=2] {'dp'}, dimensions={0}, use_global_device_ids=true | all-gather | bytes 1536 | tf_op jit(solution)/shard_map/all_gather | solution.py:149
  24.9 0.1 copy.25
  25.0 0.2 reduce-window.16
  25.1 0.1 reduce
  25.3 0.0 copy-done.2
  25.3 9.7 %all-gather.1 = bf16[1,128,2048]{2,1,0:T(8,128)(2,1)S(1)} all-gather(bf16[1,128,512]{2,1,0:T(8,128)(2,1)S(1)} %copy-done.2), channel_id=3, replica_groups=mesh['section'=4,'expert'=4,'dp'=2] {'expert'}, dimensions={2}, use_global_device_ids=true | all-gather | bytes 655360 | tf_op jit(solution)/shard_map/all_gather | solution.py:100
  34.9 0.2 convolution_convert_fusion
  35.2 0.2 convolution_convert_fusion.1
  35.4 2.3 %all_gather.23 = bf16[160,2048]{1,0:T(8,128)(2,1)S(1)} all-gather(bf16[80,2048]{1,0:T(8,128)(2,1)S(1)} %convolution_convert_fusion.1), channel_id=1, replica_groups=mesh['section'=4,'expert'=4,'dp'=2] {'dp'}, dimensions={0}, use_global_device_ids=true | all-gather | bytes 983040 | tf_op jit(solution)/shard_map/all_gather | solution.py:145
  37.7 2.3 %all_gather.24 = bf16[160,2048]{1,0:T(8,128)(2,1)S(1)} all-gather(bf16[80,2048]{1,0:T(8,128)(2,1)S(1)} %convolution_convert_fusion), channel_id=1, replica_groups=mesh['section'=4,'expert'=4,'dp'=2] {'dp'}, dimensions={0}, use_global_device_ids=true | all-gather | bytes 983040 | tf_op jit(solution)/shard_map/all_gather | solution.py:144
  40.0 9.3 %fusion.2 = f32[160,3584]{1,0:T(8,128)} fusion(bf16[160,2048]{1,0:T(8,128)(2,1)S(1)} %all_gather.24, bf16[1,2048,3584]{2,1,0:T(8,128)(2,1)} %param.17), kind=kOutput, calls=%fused_computation.2 | convolution fusion | flops 2348810240 | bytes 17629184 | tf_op jit(solution)/shard_map/dot_general | solution.py:61
  49.3 0.9 copy-done.1
  50.1 3.9 %fusion.6 = f32[160,3584]{1,0:T(8,128)} fusion(bf16[160,2048]{1,0:T(8,128)(2,1)S(1)} %all_gather.24, bf16[1,2048,3584]{2,1,0:T(8,128)(2,1)S(1)} %copy-done.1), kind=kOutput, calls=%fused_computation.6 | convolution fusion | flops 2348810240 | bytes 17629184 | tf_op jit(solution)/shard_map/dot_general | solution.py:62
  54.1 11.6 %fusion.10 = f32[160,3584]{1,0:T(8,128)} fusion(bf16[160,2048]{1,0:T(8,128)(2,1)S(1)} %all_gather.23, bf16[1,3584,2048]{2,1,0:T(8,128)(2,1)} %param.19), kind=kOutput, calls=%fused_computation.10 | convolution fusion | flops 2348810240 | bytes 17629184 | tf_op jit(solution)/shard_map/dot_general | solution.py:68
  65.7 12.1 %fusion = f32[160,2048]{1,0:T(8,128)S(1)} fusion(bf16[1,2048,3584]{2,1,0:T(8,128)(2,1)} %param.17, f32[160,3584]{1,0:T(8,128)} %fusion.2, f32[160,3584]{1,0:T(8,128)} %fusion.10, f32[160,3584]{1,0:T(8,128)} %fusion.6), kind=kOutput, calls=%fused_computation | convolution fusion | flops 2354544640 | bytes 22872064 | tf_op jit(solution)/shard_map/dot_general | solution.py:71
  77.8 12.7 %fusion.15 = f32[160,2048]{1,0:T(8,128)} fusion(f32[160,2048]{1,0:T(8,128)S(1)} %fusion, bf16[1,2048,3584]{2,1,0:T(8,128)(2,1)} %param.18, f32[160,3584]{1,0:T(8,128)} %fusion.10, f32[160,3584]{1,0:T(8,128)} %fusion.2), kind=kOutput, calls=%fused_computation.13 | convolution fusion | flops 2352578560 | bytes 21889024 | tf_op jit(solution)/shard_map/dot_general | solution.py:71
  90.5 2.2 %reshape.159 = f32[2,80,4,512]{3,2,1,0:T(4,128)S(1)} reshape(f32[160,2048]{1,0:T(8,128)} %fusion.15) | data formatting | bytes 2621440 | tf_op jit(solution)/shard_map/reshape | solution.py:154
  92.7 0.3 reduce_window_sum.25
  93.0 1.8 %all-gather.4 = f32[2,1,128]{2,1,0:T(1,128)S(1)} all-gather(f32[1,1,128]{2,1,0:T(1,128)S(1)} %bitcast.143), channel_id=1, replica_groups=mesh['section'=4,'expert'=4,'dp'=2] {'dp'}, dimensions={0}, use_global_device_ids=true | all-gather | bytes 1536 | tf_op jit(solution)/shard_map/all_gather | solution.py:150
  94.8 1.5 multiply_bitcast_fusion
  96.4 0.0 copy-start.6
  96.4 0.0 copy-start.3
  96.4 1.6 copy.28
  98.0 0.0 reduce-scatter.2.cloned.1.call-update
  98.0 0.0 all-reduce.5.cloned.1.call-start
  98.1 0.0 copy-done.6
  98.1 0.2 reduce-window.17
  98.2 0.0 copy-done
  98.3 0.2 fusion.48
  98.4 15.4 %psum.35 = f32[128,64]{0,1:T(8,128)S(1)} all-reduce(f32[128,64]{0,1:T(8,128)S(1)} %fusion.48), channel_id=1, replica_groups=mesh['section'=4,'expert'=4,'dp'=2] {'expert'}, use_global_device_ids=true, to_apply=%region_10.11 | all-reduce | flops 8192 | bytes 65536 | tf_op jit(solution)/shard_map/psum | solution.py:125
  113.8 0.0 copy-done.3
  113.8 9.4 %all-gather.2 = bf16[1,2048,64]{1,2,0:T(8,128)(2,1)S(1)} all-gather(bf16[1,512,64]{1,2,0:T(8,128)(2,1)S(1)} %copy-done.3), channel_id=4, replica_groups=mesh['section'=4,'expert'=4,'dp'=2] {'expert'}, dimensions={1}, use_global_device_ids=true | all-gather | bytes 327680 | tf_op jit(solution)/shard_map/all_gather | solution.py:123
  123.2 0.1 convert_reduce_fusion
  123.3 0.9 convolution_bitcast_fusion
  124.2 1.1 fusion.30
  125.3 0.0 all-reduce.5.cloned.1.call-update
  125.3 0.0 copy-start.5
  125.3 0.0 copy-start.7
  125.3 9.5 %fusion.20 = f32[160]{0:T(256)S(1)} fusion(bf16[1,3584,2048]{2,1,0:T(8,128)(2,1)} %param.19, bf16[160,2048]{1,0:T(8,128)(2,1)S(1)} %all_gather.23, f32[160,3584]{1,0:T(8,128)} %fusion.6, f32[160,3584]{1,0:T(8,128)} %fusion.2), kind=kOutput, calls=%fused_computation.23 | convolution fusion | flops 2353233664 | bytes 19923584 | tf_op jit(solution)/shard_map/dot_general | solution.py:66
  134.9 0.0 copy-start.4
  134.9 0.1 convert_element_type.123
  135.0 2.5 %all-reduce = f32[160]{0:T(256)S(1)} all-reduce(f32[160]{0:T(256)S(1)} %fusion.20), channel_id=6, replica_groups=mesh['section'=4,'expert'=4,'dp'=2] {'dp'}, use_global_device_ids=true, to_apply=%region_12.13.clone | all-reduce | flops 160 | bytes 1280
  137.5 0.6 dynamic-slice.3
  138.7 0.2 convolution_bitcast_fusion.1
  138.9 0.1 broadcast_multiply_fusion
  139.0 1.3 reduce-scatter.2.cloned.1.call-done
  140.3 1.3 fusion.47
  141.6 8.9 %all-reduce.1 = (f32[128,1]{0,1:T(1,128)S(1)}, f32[128,4]{0,1:T(4,128)S(1)}) all-reduce(f32[128,1]{0,1:T(1,128)S(1)} %bitcast.140, f32[128,4]{0,1:T(4,128)S(1)} %broadcast_multiply_fusion), channel_id=1, replica_groups=mesh['section'=4,'expert'=4,'dp'=2] {'expert'}, use_global_device_ids=true, to_apply=%region_17.18 | all-reduce | flops 640 | bytes 5120 | tf_op jit(solution)/shard_map/psum | solution.py:171
  150.6 0.7 fusion.32
  151.3 0.4 fusion.28
  151.6 3.4 %collective-permute-start = (bf16[128,512]{1,0:T(8,128)(2,1)S(1)}, bf16[128,512]{1,0:T(8,128)(2,1)S(1)}, u32[]{:S(2)}, u32[]{:S(2)}) collective-permute-start(bf16[128,512]{1,0:T(8,128)(2,1)S(1)} %fusion.28), channel_id=1, source_target_pairs={{8,0},{16,8},{24,16},{0,24},{9,1},{17,9},{25,17},{1,25},{10,2},{18... | collective-permute-start | bytes 393224 | tf_op jit(solution)/shard_map/ppermute | solution.py:18
  155.1 2.5 %collective-permute-done = bf16[128,512]{1,0:T(8,128)(2,1)S(1)} collective-permute-done((bf16[128,512]{1,0:T(8,128)(2,1)S(1)}, bf16[128,512]{1,0:T(8,128)(2,1)S(1)}, u32[]{:S(2)}, u32[]{:S(2)}) %collective-permute-start) | collective-permute-done | bytes 131104 | tf_op jit(solution)/shard_map/ppermute | solution.py:18
  157.6 0.7 copy.35
  158.2 1.6 copy.36
  159.8 1.6 copy.37
  (20 shorter events, 0.1 us)
Async XLA Ops:
  8.0 90.3 %copy-start = (bf16[1,64,512]{2,1,0:T(8,128)(2,1)S(1)}, bf16[1,64,512]{2,1,0:T(8,128)(2,1)}, u32[]{:S(2)}) copy-start(bf16[1,64,512]{2,1,0:T(8,128)(2,1)} %param.21) | copy-start | bytes 196612
  8.0 17.2 %copy-start.2 = (bf16[1,128,512]{2,1,0:T(8,128)(2,1)S(1)}, bf16[1,128,512]{2,1,0:T(8,128)(2,1)}, u32[]{:S(2)}) copy-start(bf16[1,128,512]{2,1,0:T(8,128)(2,1)} %param.12) | copy-start | bytes 393220
  8.0 132.3 %reduce-scatter.2.cloned.1.call-start = ((), (), s32[]{:S(2)}) async-start(), calls=%async_computation.1 | async-start | bytes 2359296 | tf_op jit(solution)/shard_map/reduce_scatter | solution.py:157
  40.0 10.2 %copy-start.1 = (bf16[1,2048,3584]{2,1,0:T(8,128)(2,1)S(1)}, bf16[1,2048,3584]{2,1,0:T(8,128)(2,1)}, u32[]{:S(2)}) copy-start(bf16[1,2048,3584]{2,1,0:T(8,128)(2,1)} %param.18) | copy-start | bytes 44040196
  96.4 1.7 %copy-start.6 = (s32[1,4]{1,0:T(1,128)S(1)}, s32[1,4]{1,0:T(1,128)}, u32[]{:S(2)}) copy-start(s32[1,4]{1,0:T(1,128)} %param.14) | copy-start | bytes 52
  96.4 17.4 %copy-start.3 = (bf16[1,512,64]{1,2,0:T(8,128)(2,1)S(1)}, bf16[1,512,64]{1,2,0:T(8,128)(2,1)}, u32[]{:S(2)}) copy-start(bf16[1,512,64]{1,2,0:T(8,128)(2,1)} %param.20) | copy-start | bytes 196612
  98.0 59.6 %all-reduce.5.cloned.1.call-start = ((), (), s32[]{:S(2)}) async-start(), calls=%async_computation.2 | async-start | bytes 524288 | tf_op jit(solution)/shard_map/psum | solution.py:136
  125.3 9.6 %copy-start.5 = (f32[1,2048]{1,0:T(1,128)S(1)}, f32[1,2048]{1,0:T(1,128)}, u32[]{:S(2)}) copy-start(f32[1,2048]{1,0:T(1,128)} %param.15) | copy-start | bytes 24580
  125.3 12.2 %copy-start.7 = (u32[32]{0:T(128)S(1)}, u32[32]{0:T(128)}, u32[]{:S(2)}) copy-start(u32[32]{0:T(128)} %constant.94) | copy-start | bytes 388
  134.9 15.7 %copy-start.4 = (bf16[1,2048,4]{1,2,0:T(4,128)(2,1)S(1)}, bf16[1,2048,4]{1,2,0:T(4,128)(2,1)}, u32[]{:S(2)}) copy-start(bf16[1,2048,4]{1,2,0:T(4,128)(2,1)} %param.16) | copy-start | bytes 49156
  151.6 6.0 %collective-permute-start = (bf16[128,512]{1,0:T(8,128)(2,1)S(1)}, bf16[128,512]{1,0:T(8,128)(2,1)S(1)}, u32[]{:S(2)}, u32[]{:S(2)}) collective-permute-start(bf16[128,512]{1,0:T(8,128)(2,1)S(1)} %fusion.28), channel_id=1, source_target_pairs={{8,0},{16,8},{24,16},{0,24},{9,1},{17,9},{25,17},{1,25},{10,2},{18... | collective-permute-start | bytes 393224 | tf_op jit(solution)/shard_map/ppermute | solution.py:18
Sparse Core Ops, SparseCore 0:
  98.1 42.1 reduce-scatter.1
Sparse Core Ops, SparseCore 1:
  125.4 18.3 all-reduce.4
where the time goes:
time: 169 us
  matrix products  66.8 us (40%)
  blocking collectives  66 us (39%)
  between operations  16.4 us (10%)
  local copies, waits for them, and re-layouts  9.96 us (6%)
  waiting for transfers between devices  3.87 us (2%)
  starting transfers between devices  3.51 us (2%)
  other arithmetic  2.28 us (1%)
    psum x1, blocking collectives, body(): lax.psum(jnp.dot(gradient_columns, backward_columns.T, preferred_element_...  15.4 us
    dot_general x1, matrix products, expert_back(): jnp.dot(d_up, expert_up_weight.T, preferred_element_type=jnp.float32)  12.7 us
    dot_general x1, matrix products, expert_back(): jnp.dot(d_gate, expert_gate_weight.T, preferred_element_type=jnp.float32)  12.1 us
    all_gather x1, blocking collectives, body(): lax.all_gather(s_cols, 'expert', axis=1, tiled=True)  12 us
    dot_general x1, matrix products, expert_back(): jnp.dot(adapter_gradient_list, expert_down_weight.T, preferred_element_ty...  11.6 us
    all_gather x1, blocking collectives, body(): lax.all_gather(gradient_columns, 'expert', axis=1, tiled=True)  9.67 us
    dot_general x1, matrix products, expert_back(): jnp.dot(hidden, expert_down_weight, preferred_element_type=jnp.float32)  9.53 us
    all_gather x1, blocking collectives, body(): a_full = lax.all_gather(down_map_rows, 'expert', axis=0, tiled=True)  9.38 us
  transfers between devices with their start and end apart: 3, of which 2 were waited for; matrix products, arithmetic and copies ran while one was open for 9% of the time, Pallas kernels for 0%

commit v1 on v0

--- a/solution.py
+++ b/solution.py
@@ -96,7 +96,9 @@
     gradient_columns = cotangent[0]
     count, width = s_cols.shape
     s_full, g_full = (
-        lax.all_gather(s_cols, "expert", axis=1, tiled=True),
+        jnp.concatenate(
+            lax.all_to_all(jnp.stack([s_cols] * lax.axis_size("expert")), "expert", 0, 0), axis=1
+        ),
         lax.all_gather(gradient_columns, "expert", axis=1, tiled=True),
     )
     norm_gain_vector = layer_norm_gains[0]

time: 169 us -> 176 us (1.041)
  blocking collectives: 66 us -> 57.7 us
  starting transfers between devices: 3.51 us -> 8.96 us
  other arithmetic: 2.28 us -> 7.15 us
  local copies, waits for them, and re-layouts: 9.96 us -> 13.4 us
    all_gather x1 -> x0, blocking collectives: 12 us -> none  [body(): lax.all_gather(s_cols, 'expert', axis=1, tiled=True)]
    all_to_all x0 -> x1, starting transfers between devices: none -> 5.19 us  [body(): lax.all_to_all(jnp.stack([s_cols] * lax.axis_size('expert')), 'expert', 0...]
    convert_element_type x0 -> x1, local copies, waits for them, and re-layouts: none -> 2.52 us  [prepare(): expert_values = whole_batch.astype(jnp.float32)]
    all_gather x1, blocking collectives: 9.67 us -> 12.2 us  [body(): lax.all_gather(gradient_columns, 'expert', axis=1, tiled=True)]
    another operation x0 -> x1, local copies, waits for them, and re-layouts: none -> 1.77 us  [body(): jnp.stack([s_cols] * lax.axis_size('expert'))]
    unnamed x20 -> x41, local copies, waits for them, and re-layouts: 5.31 us -> 4.97 us
  transfers between devices with their start and end apart: 3 -> 4, of which waited for: 2 -> 2; matrix products, arithmetic and copies ran while one was open for 9% -> 11% of each run, Pallas kernels for 0% -> 0%
where the time goes in v1:
time: 176 us; the launch traced here: 175 us
  matrix products  68.1 us (39%)
  blocking collectives  57.7 us (33%)
  between operations  16.5 us (9%)
  local copies, waits for them, and re-layouts  13.4 us (8%)
  starting transfers between devices  8.96 us (5%)
  other arithmetic  7.15 us (4%)
  waiting for transfers between devices  3.51 us (2%)
    psum x1, blocking collectives, body(): lax.psum(jnp.dot(gradient_columns, backward_columns.T, preferred_element_...  15.3 us
    dot_general x1, matrix products, expert_back(): jnp.dot(d_up, expert_up_weight.T, preferred_element_type=jnp.float32)  12.8 us
    all_gather x1, blocking collectives, body(): lax.all_gather(gradient_columns, 'expert', axis=1, tiled=True)  12.2 us
    dot_general x1, matrix products, expert_back(): jnp.dot(d_gate, expert_gate_weight.T, preferred_element_type=jnp.float32)  12.1 us
    dot_general x1, matrix products, expert_back(): jnp.dot(adapter_gradient_list, expert_down_weight.T, preferred_element_ty...  11.6 us
    all_gather x1, blocking collectives, body(): a_full = lax.all_gather(down_map_rows, 'expert', axis=0, tiled=True)  10.2 us
    dot_general x1, matrix products, expert_back(): jnp.dot(hidden, expert_down_weight, preferred_element_type=jnp.float32)  10.1 us
    dot_general x1, matrix products, expert_back(): gate = jnp.dot(rows, expert_gate_weight, preferred_element_type=jnp.float32)  9.28 us
  transfers between devices with their start and end apart: 4, of which 2 were waited for; matrix products, arithmetic and copies ran while one was open for 11% of the time, Pallas kernels for 0%

profile of v1, /device:TPU:0, one launch (start us, length us, event | category | flops | bytes accessed | tf_op | source)
XLA Modules:
  0.0 175.3 jit_solution(2333270980339822736)
XLA Ops:
  8.0 0.0 copy-start
  8.0 1.8 %stack.3 = bf16[4,128,512]{2,1,0:T(8,128)(2,1)} broadcast(bf16[128,512]{1,0:T(8,128)(2,1)} %bitcast.122), dimensions={1,2} | broadcast | bytes 655360 | tf_op jit(solution)/shard_map/stack | solution.py:100
  9.8 5.2 %all-to-all-start = ((bf16[4,128,512]{2,1,0:T(8,128)(2,1)}), bf16[4,128,512]{2,1,0:T(8,128)(2,1)S(1)}, u32[]{:S(2)}, u32[]{:S(2)}) async-start(bf16[4,128,512]{2,1,0:T(8,128)(2,1)} %stack.3), calls=%async_computation | async-start | bytes 1048576 | tf_op jit(solution)/shard_map/all_to_all | solution.py:100
  15.0 0.5 broadcast.159
  15.5 1.4 reduce.6
  16.9 12.2 %all-gather = bf16[1,128,2048]{2,1,0:T(8,128)(2,1)S(1)} all-gather(bf16[1,128,512]{2,1,0:T(8,128)(2,1)} %param.12), channel_id=2, replica_groups=mesh['section'=4,'expert'=4,'dp'=2] {'expert'}, dimensions={2}, use_global_device_ids=true | all-gather | bytes 655360 | tf_op jit(solution)/shard_map/all_gather | solution.py:102
  29.1 0.3 copy.32
  29.4 0.0 copy-start.5
  29.4 0.3 multiply_reduce_fusion
  29.7 1.1 convert_element_type.117
  30.7 1.4 convert_multiply_fusion
  32.1 0.2 select_reduce_fusion.2
  32.3 0.1 multiply_reduce_fusion.2
  32.4 1.8 %all-gather.2 = f32[2,1,128]{2,1,0:T(1,128)S(1)} all-gather(f32[1,1,128]{2,1,0:T(1,128)S(1)} %bitcast.133), channel_id=1, replica_groups=mesh['section'=4,'expert'=4,'dp'=2] {'dp'}, dimensions={0}, use_global_device_ids=true | all-gather | bytes 1536 | tf_op jit(solution)/shard_map/all_gather | solution.py:151
  34.3 2.5 %copy.39 = f32[128,2048]{1,0:T(8,128)} copy(f32[128,2048]{0,1:T(8,128)} %bitcast.120) | data formatting | bytes 2097152 | tf_op jit(solution)/shard_map/convert_element_type | solution.py:32
  36.8 1.8 %all-gather.3 = f32[2,1,128]{2,1,0:T(1,128)S(1)} all-gather(f32[1,1,128]{2,1,0:T(1,128)S(1)} %bitcast.134), channel_id=1, replica_groups=mesh['section'=4,'expert'=4,'dp'=2] {'dp'}, dimensions={0}, use_global_device_ids=true | all-gather | bytes 1536 | tf_op jit(solution)/shard_map/all_gather | solution.py:152
  38.6 0.3 reduce_window_sum.25
  38.9 0.1 copy.33
  39.0 0.2 reduce-window.16
  39.2 0.1 reduce.2
  39.3 1.4 multiply_convert_fusion.7
  40.7 0.2 convolution_convert_fusion
  41.0 0.0 slice-start.1
  41.0 0.2 convolution_convert_fusion.1
  41.2 2.4 %all_gather.19 = bf16[160,2048]{1,0:T(8,128)(2,1)S(1)} all-gather(bf16[80,2048]{1,0:T(8,128)(2,1)S(1)} %convolution_convert_fusion.1), channel_id=1, replica_groups=mesh['section'=4,'expert'=4,'dp'=2] {'dp'}, dimensions={0}, use_global_device_ids=true | all-gather | bytes 983040 | tf_op jit(solution)/shard_map/all_gather | solution.py:147
  43.6 2.4 %all_gather.20 = bf16[160,2048]{1,0:T(8,128)(2,1)S(1)} all-gather(bf16[80,2048]{1,0:T(8,128)(2,1)S(1)} %convolution_convert_fusion), channel_id=1, replica_groups=mesh['section'=4,'expert'=4,'dp'=2] {'dp'}, dimensions={0}, use_global_device_ids=true | all-gather | bytes 983040 | tf_op jit(solution)/shard_map/all_gather | solution.py:146
  46.1 9.3 %fusion.2 = f32[160,3584]{1,0:T(8,128)} fusion(bf16[160,2048]{1,0:T(8,128)(2,1)S(1)} %all_gather.20, bf16[1,2048,3584]{2,1,0:T(8,128)(2,1)} %param.17), kind=kOutput, calls=%fused_computation.2 | convolution fusion | flops 2348810240 | bytes 17629184 | tf_op jit(solution)/shard_map/dot_general | solution.py:61
  55.4 3.9 %fusion.6 = f32[160,3584]{1,0:T(8,128)} fusion(bf16[160,2048]{1,0:T(8,128)(2,1)S(1)} %all_gather.20, bf16[1,2048,3584]{2,1,0:T(8,128)(2,1)S(1)} %bitcast.117), kind=kOutput, calls=%fused_computation.6 | convolution fusion | flops 2348810240 | bytes 17629184 | tf_op jit(solution)/shard_map/dot_general | solution.py:62
  59.3 11.6 %fusion.10 = f32[160,3584]{1,0:T(8,128)} fusion(bf16[160,2048]{1,0:T(8,128)(2,1)S(1)} %all_gather.19, bf16[1,3584,2048]{2,1,0:T(8,128)(2,1)} %param.19), kind=kOutput, calls=%fused_computation.10 | convolution fusion | flops 2348810240 | bytes 17629184 | tf_op jit(solution)/shard_map/dot_general | solution.py:68
  70.9 12.1 %fusion = f32[160,2048]{1,0:T(8,128)S(1)} fusion(bf16[1,2048,3584]{2,1,0:T(8,128)(2,1)} %param.17, f32[160,3584]{1,0:T(8,128)} %fusion.2, f32[160,3584]{1,0:T(8,128)} %fusion.10, f32[160,3584]{1,0:T(8,128)} %fusion.6), kind=kOutput, calls=%fused_computation | convolution fusion | flops 2354544640 | bytes 22872064 | tf_op jit(solution)/shard_map/dot_general | solution.py:71
  83.1 12.8 %fusion.15 = f32[160,2048]{1,0:T(8,128)} fusion(f32[160,2048]{1,0:T(8,128)S(1)} %fusion, bf16[1,2048,3584]{2,1,0:T(8,128)(2,1)} %param.18, f32[160,3584]{1,0:T(8,128)} %fusion.10, f32[160,3584]{1,0:T(8,128)} %fusion.2), kind=kOutput, calls=%fused_computation.13 | convolution fusion | flops 2352578560 | bytes 21889024 | tf_op jit(solution)/shard_map/dot_general | solution.py:71
  95.8 2.2 %reshape.181 = f32[2,80,4,512]{3,2,1,0:T(4,128)S(1)} reshape(f32[160,2048]{1,0:T(8,128)} %fusion.15) | data formatting | bytes 2621440 | tf_op jit(solution)/shard_map/reshape | solution.py:156
  98.0 1.5 multiply_bitcast_fusion
  99.5 0.0 copy-start.12
  99.5 0.0 copy-start.13
  99.6 0.0 copy-start.3
  99.6 0.0 copy-start.4
  99.6 1.6 copy.37
  101.2 0.0 reduce-scatter.2.cloned.1.call-update
  101.2 0.0 all-reduce.5.cloned.1.call-start
  101.3 0.2 reduce-window.17
  101.4 0.6 dynamic-slice.2
  102.7 0.2 fusion.38
  102.9 15.3 %psum.35 = f32[128,64]{0,1:T(8,128)S(1)} all-reduce(f32[128,64]{0,1:T(8,128)S(1)} %fusion.38), channel_id=1, replica_groups=mesh['section'=4,'expert'=4,'dp'=2] {'expert'}, use_global_device_ids=true, to_apply=%region_10.11 | all-reduce | flops 8192 | bytes 65536 | tf_op jit(solution)/shard_map/psum | solution.py:127
  118.2 10.2 %all-gather.1 = bf16[1,2048,64]{1,2,0:T(8,128)(2,1)} all-gather(bf16[1,512,64]{1,2,0:T(8,128)(2,1)S(1)} %copy-done.4), channel_id=3, replica_groups=mesh['section'=4,'expert'=4,'dp'=2] {'expert'}, dimensions={1}, use_global_device_ids=true | all-gather | bytes 327680 | tf_op jit(solution)/shard_map/all_gather | solution.py:125
  128.4 0.1 convert_reduce_fusion
  128.5 10.1 %fusion.20 = f32[160]{0:T(256)} fusion(bf16[1,3584,2048]{2,1,0:T(8,128)(2,1)} %param.19, bf16[160,2048]{1,0:T(8,128)(2,1)S(1)} %all_gather.19, f32[160,3584]{1,0:T(8,128)} %fusion.6, f32[160,3584]{1,0:T(8,128)} %fusion.2), kind=kOutput, calls=%fused_computation.23 | convolution fusion | flops 2353233664 | bytes 19923584 | tf_op jit(solution)/shard_map/dot_general | solution.py:66
  138.6 2.6 %all-reduce = f32[160]{0:T(256)S(1)} all-reduce(f32[160]{0:T(256)} %fusion.20), channel_id=5, replica_groups=mesh['section'=4,'expert'=4,'dp'=2] {'dp'}, use_global_device_ids=true, to_apply=%region_12.13.clone | all-reduce | flops 160 | bytes 1280
  141.2 0.8 convolution_bitcast_fusion.1
  142.1 0.9 convolution_bitcast_fusion
  142.9 2.1 %fusion.30 = f32[1,64,512]{2,1,0:T(8,128)} fusion(bf16[128,2048]{1,0:T(8,128)(2,1)S(1)} %multiply_convert_fusion.7, bf16[1,2048,64]{1,2,0:T(8,128)(2,1)} %all-gather.1, bf16[1,128,512]{2,1,0:T(8,128)(2,1)S(1)} %copy-done.3, s32[128]{0:T(128)S(1)} %convert_reduce_fusion, s32[64]{0:T(128)S(1)} %and_select_fusion), kind=kOutput, calls=%fused_computation.35 | convolution fusion | flops 42000384 | bytes 1049344 | tf_op jit(solution)/shard_map/dot_general | solution.py:132
  145.0 0.7 broadcast_multiply_fusion
  145.7 0.0 all-reduce.5.cloned.1.call-update
  145.7 0.0 reduce-scatter.2.cloned.1.call-done
  145.7 1.4 multiply_reduce_fusion.1
  147.1 8.9 %all-reduce.1 = (f32[128,1]{0,1:T(1,128)S(1)}, f32[128,4]{0,1:T(4,128)S(1)}) all-reduce(f32[128,1]{0,1:T(1,128)S(1)} %bitcast.130, f32[128,4]{0,1:T(4,128)S(1)} %broadcast_multiply_fusion), channel_id=1, replica_groups=mesh['section'=4,'expert'=4,'dp'=2] {'expert'}, use_global_device_ids=true, to_apply=%region_17.18 | all-reduce | flops 640 | bytes 5120 | tf_op jit(solution)/shard_map/psum | solution.py:173
  156.1 0.5 fusion.32
  156.5 0.4 fusion.28
  156.9 3.7 %collective-permute-start = (bf16[128,512]{1,0:T(8,128)(2,1)S(1)}, bf16[128,512]{1,0:T(8,128)(2,1)S(1)}, u32[]{:S(2)}, u32[]{:S(2)}) collective-permute-start(bf16[128,512]{1,0:T(8,128)(2,1)S(1)} %fusion.28), channel_id=1, source_target_pairs={{8,0},{16,8},{24,16},{0,24},{9,1},{17,9},{25,17},{1,25},{10,2},{18... | collective-permute-start | bytes 393224 | tf_op jit(solution)/shard_map/ppermute | solution.py:18
  160.6 2.5 %collective-permute-done = bf16[128,512]{1,0:T(8,128)(2,1)S(1)} collective-permute-done((bf16[128,512]{1,0:T(8,128)(2,1)S(1)}, bf16[128,512]{1,0:T(8,128)(2,1)S(1)}, u32[]{:S(2)}, u32[]{:S(2)}) %collective-permute-start) | collective-permute-done | bytes 131104 | tf_op jit(solution)/shard_map/ppermute | solution.py:18
  163.2 0.9 all-reduce.5.cloned.1.call-done
  164.1 0.7 copy.45
  164.7 1.6 copy.46
  166.3 1.6 copy.47
  (49 shorter events, 0.2 us)
Async XLA Ops:
  8.0 94.7 %copy-start = (bf16[1,64,512]{2,1,0:T(8,128)(2,1)S(1)}, bf16[1,64,512]{2,1,0:T(8,128)(2,1)}, u32[]{:S(2)}) copy-start(bf16[1,64,512]{2,1,0:T(8,128)(2,1)} %param.21) | copy-start | bytes 196612
  8.0 21.1 %copy-start.11 = (s32[1,128,2]{1,2,0:T(2,128)S(1)}, s32[1,128,2]{1,2,0:T(2,128)}, u32[]{:S(2)}) copy-start(s32[1,128,2]{1,2,0:T(2,128)} %param.13) | copy-start | bytes 3076
  9.8 19.3 %all-to-all-start = ((bf16[4,128,512]{2,1,0:T(8,128)(2,1)}), bf16[4,128,512]{2,1,0:T(8,128)(2,1)S(1)}, u32[]{:S(2)}, u32[]{:S(2)}) async-start(bf16[4,128,512]{2,1,0:T(8,128)(2,1)} %stack.3), calls=%async_computation | async-start | bytes 1048576 | tf_op jit(solution)/shard_map/all_to_all | solution.py:100
  15.0 130.7 %reduce-scatter.2.cloned.1.call-start = ((), (), s32[]{:S(2)}) async-start(), calls=%async_computation.2 | async-start | bytes 2359296 | tf_op jit(solution)/shard_map/reduce_scatter | solution.py:159
  29.1 3.3 %copy-start.7 = (f32[4]{0:T(128)}, f32[4]{0:T(128)S(1)}, u32[]{:S(2)}) copy-start(f32[4]{0:T(128)S(1)} %compare_convert_fusion) | copy-start | bytes 52
  29.4 2.7 %copy-start.5 = (bf16[1,2048,4]{1,2,0:T(4,128)(2,1)S(1)}, bf16[1,2048,4]{1,2,0:T(4,128)(2,1)}, u32[]{:S(2)}) copy-start(bf16[1,2048,4]{1,2,0:T(4,128)(2,1)} %param.16) | copy-start | bytes 49156
  30.7 8.6 %copy-start.6 = (f32[1,2048]{1,0:T(1,128)S(1)}, f32[1,2048]{1,0:T(1,128)}, u32[]{:S(2)}) copy-start(f32[1,2048]{1,0:T(1,128)} %param.15) | copy-start | bytes 24580
  30.7 24.6 %slice-start = ((s8[14680064]{0:T(1024)(128)(4,1)}), s8[2097152]{0:T(1024)(128)(4,1)S(1)}, s32[]{:S(2)}) async-start(s8[14680064]{0:T(1024)(128)(4,1)} %bitcast.116), calls=%async_computation.4 | async-start | bytes 4194304
  32.4 8.5 %copy-start.8 = (pred[128]{0:T(512)(128)(4,1)}, pred[128]{0:T(512)(128)(4,1)S(1)}, u32[]{:S(2)}) copy-start(pred[128]{0:T(512)(128)(4,1)S(1)} %convert_compare_fusion) | copy-start | bytes 388
  39.3 1.7 copy-start.10
  41.0 14.4 %slice-start.1 = ((s8[14680064]{0:T(1024)(128)(4,1)}), s8[4194304]{0:T(1024)(128)(4,1)S(1)}, s32[]{:S(2)}) async-start(s8[14680064]{0:T(1024)(128)(4,1)} %bitcast.116), calls=%async_computation.5 | async-start | bytes 8388608
  46.1 9.3 %slice-start.2 = ((s8[14680064]{0:T(1024)(128)(4,1)}), s8[4194304]{0:T(1024)(128)(4,1)S(1)}, s32[]{:S(2)}) async-start(s8[14680064]{0:T(1024)(128)(4,1)} %bitcast.116), calls=%async_computation.6 | async-start | bytes 8388608
  46.1 9.3 %slice-start.3 = ((s8[14680064]{0:T(1024)(128)(4,1)}), s8[4194304]{0:T(1024)(128)(4,1)S(1)}, s32[]{:S(2)}) async-start(s8[14680064]{0:T(1024)(128)(4,1)} %bitcast.116), calls=%async_computation.7 | async-start | bytes 8388608
  99.5 1.7 copy-start.12
  99.5 1.9 %copy-start.13 = (u32[32]{0:T(128)S(1)}, u32[32]{0:T(128)}, u32[]{:S(2)}) copy-start(u32[32]{0:T(128)} %constant.93) | copy-start | bytes 388
  99.6 3.1 %copy-start.3 = (bf16[1,128,512]{2,1,0:T(8,128)(2,1)S(1)}, bf16[1,128,512]{2,1,0:T(8,128)(2,1)}, u32[]{:S(2)}) copy-start(bf16[1,128,512]{2,1,0:T(8,128)(2,1)} %param.12) | copy-start | bytes 393220
  99.6 18.6 %copy-start.4 = (bf16[1,512,64]{1,2,0:T(8,128)(2,1)S(1)}, bf16[1,512,64]{1,2,0:T(8,128)(2,1)}, u32[]{:S(2)}) copy-start(bf16[1,512,64]{1,2,0:T(8,128)(2,1)} %param.20) | copy-start | bytes 196612
  101.2 62.9 %all-reduce.5.cloned.1.call-start = ((), (), s32[]{:S(2)}) async-start(), calls=%async_computation.3 | async-start | bytes 524288 | tf_op jit(solution)/shard_map/psum | solution.py:138
  128.5 12.7 %copy-start.9 = (pred[128]{0:T(512)(128)(4,1)S(1)}, pred[128]{0:T(512)(128)(4,1)}, u32[]{:S(2)}) copy-start(pred[128]{0:T(512)(128)(4,1)} %copy-done.8) | copy-start | bytes 388
  128.5 17.2 %copy-start.1 = (f32[128,2048]{1,0:T(8,128)S(1)}, f32[128,2048]{1,0:T(8,128)}, u32[]{:S(2)}) copy-start(f32[128,2048]{1,0:T(8,128)} %copy.39) | copy-start | bytes 3145732
  138.6 17.4 %copy-start.2 = (f32[4,128,512]{1,2,0:T(8,128)S(1)}, f32[4,128,512]{1,2,0:T(8,128)}, u32[]{:S(2)}) copy-start(f32[4,128,512]{1,2,0:T(8,128)} %get-tuple-element.15) | copy-start | bytes 3145732
  156.9 6.2 %collective-permute-start = (bf16[128,512]{1,0:T(8,128)(2,1)S(1)}, bf16[128,512]{1,0:T(8,128)(2,1)S(1)}, u32[]{:S(2)}, u32[]{:S(2)}) collective-permute-start(bf16[128,512]{1,0:T(8,128)(2,1)S(1)} %fusion.28), channel_id=1, source_target_pairs={{8,0},{16,8},{24,16},{0,24},{9,1},{17,9},{25,17},{1,25},{10,2},{18... | collective-permute-start | bytes 393224 | tf_op jit(solution)/shard_map/ppermute | solution.py:18
Sparse Core Ops, SparseCore 0:
  101.3 42.1 reduce-scatter.1
Sparse Core Ops, SparseCore 1:
  145.8 18.2 all-reduce.4
